TPU v7x, 32 devices: a whole 2x2x4 slice. The times are simulated.
32 devices in a mesh: gx: 4 (over y, core), gy: 2 (over x), gz: 4 (over z).
Axes of the slice: x: 2, y: 2, z: 4, core: 2. Of those that a mesh axis runs over, the one named last changes fastest.
Arguments:
- source: float32 [256, 128, 128], P('gx', 'gy', 'gz'), may hold values from -6 to 6
- green: float32 [512, 256, 256], P(None, ('gx', 'gz'), 'gy'), may hold values from 0.05 to 2, as said below
Outputs:
- potential: float32 [256, 128, 128], P('gx', 'gy', 'gz')
Inputs may be any that keep to these rules, and one draw needn't show every extreme that they name: `green`: greenfull is even: greenfull[k] equals greenfull at (-k1 mod 512, -k2 mod 256, -k3 mod 256).
All inputs are finite; a program needn't handle non-finite values.
Results may differ from a plain program's by a relative error of at most 0.00007.
Values sent between devices are 32-bit elements; how exact they have to be, the bound alone decides.
A program may use at most 128 MiB of HBM per device.

v0:
```python
import math

import jax
import jax.numpy as jnp
from jax import lax
from jax.sharding import PartitionSpec as P


def phase_table(row_index, column_index, length):
    phase_index = row_index[:, None] * column_index[None, :] % length
    angles = phase_index.astype(jnp.float32) * (2.0 * math.pi / length)
    return (jnp.cos(angles), jnp.sin(angles))


def pair_frequency(position, length):
    unit_index = position // 2
    member = position % 2
    return jnp.where(
        unit_index == 0,
        member * (length // 2),
        jnp.where(member == 0, unit_index, length - unit_index),
    )


def product(form, left, table):
    return jnp.einsum(form, left, table, precision=lax.Precision.HIGHEST)


def mirror_plane(field, first_block):
    flipped = jnp.roll(jnp.flip(field, 1), 1, 1)
    count_y, count_x = field.shape
    swapped = flipped.reshape(count_y // 2, 2, count_x)[:, ::-1, :].reshape(count_y, count_x)
    local_row = lax.iota(jnp.int32, count_y)
    keep_unit = jnp.logical_and(first_block, local_row < 2)
    return jnp.where(keep_unit[:, None], flipped, swapped)


def per_device(source, green):
    size_gx = lax.axis_size("gx")
    size_gy = lax.axis_size("gy")
    size_gz = lax.axis_size("gz")
    brick_x, brick_y, brick_z = source.shape
    grid_x = brick_x * size_gx
    grid_y = brick_y * size_gy
    grid_z = brick_z * size_gz
    long_x = 2 * grid_x
    long_y = 2 * grid_y
    long_z = 2 * grid_z
    cell_z = lax.iota(jnp.int32, grid_z)
    parity_sign = (1 - 2 * (cell_z % 2)).astype(jnp.float32)
    z_lines = lax.all_to_all(source, "gz", split_axis=0, concat_axis=2, tiled=True)
    kept_freq = lax.iota(jnp.int32, long_z // 2)
    z_cos, z_sin = phase_table(cell_z, kept_freq, long_z)
    z_sin = jnp.where(kept_freq[None, :] == 0, -parity_sign[:, None], z_sin)
    z_real = product("abn,nk->abk", z_lines, z_cos)
    z_imag = -product("abn,nk->abk", z_lines, z_sin)
    y_real, y_imag = (
        lax.all_to_all(z_real, "gy", split_axis=2, concat_axis=1, tiled=True),
        lax.all_to_all(z_imag, "gy", split_axis=2, concat_axis=1, tiled=True),
    )
    y_cos, y_sin = phase_table(
        lax.iota(jnp.int32, grid_y), pair_frequency(lax.iota(jnp.int32, long_y), long_y), long_y
    )
    fy_real = product("ayc,yk->ack", y_real, y_cos) + product("ayc,yk->ack", y_imag, y_sin)
    fy_imag = product("ayc,yk->ack", y_imag, y_cos) - product("ayc,yk->ack", y_real, y_sin)
    x_real, x_imag = (
        lax.all_to_all(fy_real, ("gx", "gz"), split_axis=2, concat_axis=0, tiled=True),
        lax.all_to_all(fy_imag, ("gx", "gz"), split_axis=2, concat_axis=0, tiled=True),
    )
    x_rows = lax.iota(jnp.int32, grid_x)
    x_cos, x_sin = phase_table(x_rows, lax.iota(jnp.int32, long_x), long_x)
    full_real = product("xck,xj->ckj", x_real, x_cos) + product("xck,xj->ckj", x_imag, x_sin)
    full_imag = product("xck,xj->ckj", x_imag, x_cos) - product("xck,xj->ckj", x_real, x_sin)
    kept_green = jnp.transpose(green[:, :, 0::2], (2, 1, 0))
    nyquist_green = jnp.transpose(green[:, :, 1], (1, 0))
    prod_real = kept_green * full_real
    prod_imag = kept_green * full_imag
    first_block = lax.axis_index("gx") * size_gz + lax.axis_index("gz") == 0
    first_slab = lax.axis_index("gy") == 0
    base_real = full_real[0]
    base_imag = full_imag[0]
    mirror_real = mirror_plane(base_real, first_block)
    mirror_imag = mirror_plane(base_imag, first_block)
    zero_real = 0.5 * (base_real + mirror_real)
    zero_imag = 0.5 * (base_imag - mirror_imag)
    nyq_real = 0.5 * (base_imag + mirror_imag)
    nyq_imag = 0.5 * (mirror_real - base_real)
    zero_green = kept_green[0]
    packed_real = zero_green * zero_real - nyquist_green * nyq_imag
    packed_imag = zero_green * zero_imag + nyquist_green * nyq_real
    slot_mask = jnp.logical_and(lax.iota(jnp.int32, prod_real.shape[0]) == 0, first_slab)
    prod_real = jnp.where(slot_mask[:, None, None], packed_real[None], prod_real)
    prod_imag = jnp.where(slot_mask[:, None, None], packed_imag[None], prod_imag)
    inv_xcos, inv_xsin = phase_table(
        lax.iota(jnp.int32, long_x), lax.iota(jnp.int32, grid_x), long_x
    )
    back_real = (
        product("ckj,jx->ckx", prod_real, inv_xcos) - product("ckj,jx->ckx", prod_imag, inv_xsin)
    ) / long_x
    back_imag = (
        product("ckj,jx->ckx", prod_imag, inv_xcos) + product("ckj,jx->ckx", prod_real, inv_xsin)
    ) / long_x
    mid_real, mid_imag = (
        lax.all_to_all(back_real, ("gx", "gz"), split_axis=2, concat_axis=1, tiled=True),
        lax.all_to_all(back_imag, ("gx", "gz"), split_axis=2, concat_axis=1, tiled=True),
    )
    y_order = lax.iota(jnp.int32, long_y)
    inv_ycos, inv_ysin = phase_table(
        pair_frequency(y_order, long_y), lax.iota(jnp.int32, grid_y), long_y
    )
    half_real = (
        product("cja,jy->cay", mid_real, inv_ycos) - product("cja,jy->cay", mid_imag, inv_ysin)
    ) / long_y
    half_imag = (
        product("cja,jy->cay", mid_imag, inv_ycos) + product("cja,jy->cay", mid_real, inv_ysin)
    ) / long_y
    last_real, last_imag = (
        lax.all_to_all(half_real, "gy", split_axis=2, concat_axis=0, tiled=True),
        lax.all_to_all(half_imag, "gy", split_axis=2, concat_axis=0, tiled=True),
    )
    kept_freq = lax.iota(jnp.int32, long_z // 2)
    base_cos, base_sin = phase_table(kept_freq, cell_z, long_z)
    inv_zcos = jnp.where(kept_freq[:, None] == 0, 1.0, 2.0 * base_cos)
    inv_zsin = jnp.where(kept_freq[:, None] == 0, -parity_sign[None, :], 2.0 * base_sin)
    result = (
        product("jab,jn->abn", last_real, inv_zcos) - product("jab,jn->abn", last_imag, inv_zsin)
    ) / long_z
    return lax.all_to_all(result, "gz", split_axis=2, concat_axis=0, tiled=True)


def solution(mesh):
    return jax.shard_map(
        per_device,
        mesh=mesh,
        in_specs=(P("gx", "gy", "gz"), P(None, ("gx", "gz"), "gy")),
        out_specs=P("gx", "gy", "gz"),
        check_vma=False,
    )
```

profile of v0, /device:TPU:0, one launch (start us, length us, event | category | flops | bytes accessed | tf_op | source)
XLA Modules:
  0.0 386.8 jit_solution(17257259140044009849)
XLA Ops:
  2.7 6.3 %all-to-all-start = ((f32[4,1,32768]{2,1,0:T(1,128)}), f32[4,1,32768]{2,1,0:T(1,128)S(1)}, u32[]{:S(2)}, u32[]{:S(2)}) async-start(f32[4,1,32768]{2,1,0:T(1,128)} %reshape.130), calls=%async_computation | async-start | bytes 1048576 | tf_op jit(solution)/shard_map/all_to_all | solution.py:51
  9.0 14.5 %all-to-all-done = f32[4,1,32768]{2,1,0:T(1,128)S(1)} async-done(((f32[4,1,32768]{2,1,0:T(1,128)}), f32[4,1,32768]{2,1,0:T(1,128)S(1)}, u32[]{:S(2)}, u32[]{:S(2)}) %all-to-all-start) | async-done | bytes 524320 | tf_op jit(solution)/shard_map/all_to_all | solution.py:51
  65.3 4.3 %all-to-all-start.3 = ((f32[16,1,16384]{2,1,0:T(1,128)}), f32[16,1,16384]{2,1,0:T(1,128)}, u32[]{:S(2)}, u32[]{:S(2)}) async-start(f32[16,1,16384]{2,1,0:T(1,128)} %reshape.136), calls=%async_computation.3 | async-start | bytes 2097152 | tf_op jit(solution)/shard_map/all_to_all | solution.py:67
  78.4 18.1 %all-to-all-done.3 = f32[16,1,16384]{2,1,0:T(1,128)} async-done(((f32[16,1,16384]{2,1,0:T(1,128)}), f32[16,1,16384]{2,1,0:T(1,128)}, u32[]{:S(2)}, u32[]{:S(2)}) %all-to-all-start.3) | async-done | bytes 1048608 | tf_op jit(solution)/shard_map/all_to_all | solution.py:67
  96.5 4.4 %all-to-all-start.4 = ((f32[16,1,16384]{2,1,0:T(1,128)}), f32[16,1,16384]{2,1,0:T(1,128)}, u32[]{:S(2)}, u32[]{:S(2)}) async-start(f32[16,1,16384]{2,1,0:T(1,128)} %reshape.138), calls=%async_computation.4 | async-start | bytes 2097152 | tf_op jit(solution)/shard_map/all_to_all | solution.py:68
  100.9 5.3 %slice.43 = f32[512,16,1]{2,1,0:T(8,128)} slice(f32[512,16,128]{2,1,0:T(8,128)} %param.3), slice={[0:512], [0:16], [1:2]} | slice | bytes 65536 | tf_op jit(solution)/shard_map/slice | solution.py:75
  106.1 73.2 %slice.37 = f32[512,16,64]{2,1,0:T(8,128)} slice(f32[512,16,128]{2,1,0:T(8,128)} %param.3), slice={[0:512:1], [0:16:1], [0:128:2]} | slice | bytes 4194304 | tf_op jit(solution)/shard_map/slice | solution.py:74
  185.9 4.4 %reduce.3 = f32[16,16384]{1,0:T(8,128)S(1)} reduce(f32[16,1,16384]{2,1,0:T(1,128)} %all-to-all-done.3, f32[]{:T(128)} %broadcast.408), dimensions={1}, to_apply=%all_to_all.142.reduce_sub_computation | reduce | bytes 2097156 | tf_op jit(solution)/shard_map/all_to_all | solution.py:67
  198.9 5.2 %fusion.22 = f32[64,16,512]{2,1,0:T(8,128)} fusion(f32[256,64,16]{0,2,1:T(8,128)S(1)} %copy.115), kind=kOutput, calls=%fused_computation.45 | convolution fusion | flops 1612447744 | bytes 3145728 | tf_op jit(solution)/shard_map/xck,xj->ckj/dot_general | solution.py:26
  204.1 5.3 %reduce.4 = f32[16,16384]{1,0:T(8,128)} reduce(f32[16,1,16384]{2,1,0:T(1,128)} %all-to-all-done.4, f32[]{:T(128)} %broadcast.408), dimensions={1}, to_apply=%all_to_all.146.reduce_sub_computation | reduce | bytes 2097156 | tf_op jit(solution)/shard_map/all_to_all | solution.py:68
  220.2 6.2 %convolution_add_fusion = f32[64,16,512]{2,1,0:T(8,128)S(1)} fusion(f32[64,16,512]{2,1,0:T(8,128)} %fusion.22, f32[256,64,16]{0,2,1:T(8,128)} %copy.119), kind=kOutput, calls=%fused_computation.3 | convolution fusion | flops 1612972032 | bytes 5242880 | tf_op jit(solution)/shard_map/xck,xj->ckj/dot_general | solution.py:26
  226.4 4.3 %fusion.20 = f32[64,16,512]{2,1,0:T(8,128)S(1)} fusion(f32[256,64,16]{0,2,1:T(8,128)S(1)} %copy-done.4), kind=kOutput, calls=%fused_computation.43 | convolution fusion | flops 1612447744 | bytes 3145728 | tf_op jit(solution)/shard_map/xck,xj->ckj/dot_general | solution.py:26
  230.8 4.6 %convolution_subtract_fusion = f32[64,16,512]{2,1,0:T(8,128)S(1)} fusion(f32[64,16,512]{2,1,0:T(8,128)S(1)} %fusion.20, f32[256,64,16]{0,2,1:T(8,128)S(1)} %copy.115), kind=kOutput, calls=%fused_computation.2 | convolution fusion | flops 1612972032 | bytes 5242880 | tf_op jit(solution)/shard_map/xck,xj->ckj/dot_general | solution.py:26
  239.1 5.5 %fusion.16 = f32[64,16,256]{2,1,0:T(8,128)S(1)} fusion(f32[64,16,512]{2,1,0:T(8,128)} %copy-done, f32[16,512]{1,0:T(8,128)S(1)} %get-tuple-element.6, pred[64]{0:T(512)(128)(4,1)S(1)} %compare_and_fusion.1, f32[512,16,64]{0,1,2:T(8,128)S(1)} %copy.147), kind=kOutput, calls=%fused_computation.39 | convolution fusion | flops 1613496320 | bytes 5275712 | tf_op jit(solution)/shard_map/ckj,jx->ckx/dot_general | solution.py:26
  244.6 3.8 fusion.1
  255.0 5.9 %all-to-all-start.5 = ((f32[16,1,16384]{2,1,0:T(1,128)}), f32[16,1,16384]{2,1,0:T(1,128)}, u32[]{:S(2)}, u32[]{:S(2)}) async-start(f32[16,1,16384]{2,1,0:T(1,128)} %reshape.140), calls=%async_computation.5 | async-start | bytes 2097152 | tf_op jit(solution)/shard_map/all_to_all | solution.py:104
  261.0 5.5 %fusion.14 = f32[64,16,256]{2,1,0:T(8,128)S(1)} fusion(f32[64,16,512]{2,1,0:T(8,128)} %copy-done.2, f32[16,512]{1,0:T(8,128)S(1)} %get-tuple-element.5, pred[64]{0:T(512)(128)(4,1)S(1)} %compare_and_fusion.1, f32[512,16,64]{0,1,2:T(8,128)S(1)} %copy.147), kind=kOutput, calls=%fused_computation.37 | convolution fusion | flops 1613496320 | bytes 5275712 | tf_op jit(solution)/shard_map/ckj,jx->ckx/dot_general | solution.py:26
  274.3 13.6 %all-to-all-done.5 = f32[16,1,16384]{2,1,0:T(1,128)} async-done(((f32[16,1,16384]{2,1,0:T(1,128)}), f32[16,1,16384]{2,1,0:T(1,128)}, u32[]{:S(2)}, u32[]{:S(2)}) %all-to-all-start.5) | async-done | bytes 1048608 | tf_op jit(solution)/shard_map/all_to_all | solution.py:104
  287.9 4.5 %all-to-all-start.6 = ((f32[16,1,16384]{2,1,0:T(1,128)}), f32[16,1,16384]{2,1,0:T(1,128)}, u32[]{:S(2)}, u32[]{:S(2)}) async-start(f32[16,1,16384]{2,1,0:T(1,128)} %reshape.142), calls=%async_computation.6 | async-start | bytes 2097152 | tf_op jit(solution)/shard_map/all_to_all | solution.py:105
  292.4 4.4 %reduce.5 = f32[16,16384]{1,0:T(8,128)S(1)} reduce(f32[16,1,16384]{2,1,0:T(1,128)} %all-to-all-done.5, f32[]{:T(128)} %broadcast.408), dimensions={1}, to_apply=%all_to_all.150.reduce_sub_computation | reduce | bytes 2097156 | tf_op jit(solution)/shard_map/all_to_all | solution.py:104
  304.9 14.2 %all-to-all-done.6 = f32[16,1,16384]{2,1,0:T(1,128)} async-done(((f32[16,1,16384]{2,1,0:T(1,128)}), f32[16,1,16384]{2,1,0:T(1,128)}, u32[]{:S(2)}, u32[]{:S(2)}) %all-to-all-start.6) | async-done | bytes 1048608 | tf_op jit(solution)/shard_map/all_to_all | solution.py:105
  319.1 5.3 %reduce.6 = f32[16,16384]{1,0:T(8,128)} reduce(f32[16,1,16384]{2,1,0:T(1,128)} %all-to-all-done.6, f32[]{:T(128)} %broadcast.408), dimensions={1}, to_apply=%all_to_all.154.reduce_sub_computation | reduce | bytes 2097156 | tf_op jit(solution)/shard_map/all_to_all | solution.py:105
  344.5 4.6 %all-to-all-done.7 = f32[2,1,65536]{2,1,0:T(1,128)S(1)} async-done(((f32[2,1,65536]{2,1,0:T(1,128)}), f32[2,1,65536]{2,1,0:T(1,128)S(1)}, u32[]{:S(2)}, u32[]{:S(2)}) %all-to-all-start.7) | async-done | bytes 524320 | tf_op jit(solution)/shard_map/all_to_all | solution.py:118
  366.4 16.0 %all_to_all.180 = f32[4,1,32768]{2,1,0:T(1,128)S(1)} all-to-all(f32[4,1,32768]{2,1,0:T(1,128)S(1)} %reshape.148), channel_id=1, replica_groups=mesh['gx'=4,'gy'=2,'gz'=4] {'gz'}, dimensions={0} | all-to-all | bytes 1048576 | tf_op jit(solution)/shard_map/all_to_all | solution.py:128
  (114 shorter events, 146.1 us)
Async XLA Ops:
  2.7 20.8 %all-to-all-start = ((f32[4,1,32768]{2,1,0:T(1,128)}), f32[4,1,32768]{2,1,0:T(1,128)S(1)}, u32[]{:S(2)}, u32[]{:S(2)}) async-start(f32[4,1,32768]{2,1,0:T(1,128)} %reshape.130), calls=%async_computation | async-start | bytes 1048576 | tf_op jit(solution)/shard_map/all_to_all | solution.py:51
  30.5 11.0 %all-to-all-start.1 = ((f32[2,1,65536]{2,1,0:T(1,128)}), f32[2,1,65536]{2,1,0:T(1,128)S(1)}, u32[]{:S(2)}, u32[]{:S(2)}) async-start(f32[2,1,65536]{2,1,0:T(1,128)} %reshape.132), calls=%async_computation.1 | async-start | bytes 1048576 | tf_op jit(solution)/shard_map/all_to_all | solution.py:58
  41.6 10.3 %all-to-all-start.2 = ((f32[2,1,65536]{2,1,0:T(1,128)}), f32[2,1,65536]{2,1,0:T(1,128)S(1)}, u32[]{:S(2)}, u32[]{:S(2)}) async-start(f32[2,1,65536]{2,1,0:T(1,128)} %reshape.134), calls=%async_computation.2 | async-start | bytes 1048576 | tf_op jit(solution)/shard_map/all_to_all | solution.py:59
  65.3 31.2 %all-to-all-start.3 = ((f32[16,1,16384]{2,1,0:T(1,128)}), f32[16,1,16384]{2,1,0:T(1,128)}, u32[]{:S(2)}, u32[]{:S(2)}) async-start(f32[16,1,16384]{2,1,0:T(1,128)} %reshape.136), calls=%async_computation.3 | async-start | bytes 2097152 | tf_op jit(solution)/shard_map/all_to_all | solution.py:67
  96.5 107.6 %all-to-all-start.4 = ((f32[16,1,16384]{2,1,0:T(1,128)}), f32[16,1,16384]{2,1,0:T(1,128)}, u32[]{:S(2)}, u32[]{:S(2)}) async-start(f32[16,1,16384]{2,1,0:T(1,128)} %reshape.138), calls=%async_computation.4 | async-start | bytes 2097152 | tf_op jit(solution)/shard_map/all_to_all | solution.py:68
  220.2 6.3 %copy-start.4 = (f32[256,64,16]{0,2,1:T(8,128)S(1)}, f32[256,64,16]{0,2,1:T(8,128)}, u32[]{:S(2)}) copy-start(f32[256,64,16]{0,2,1:T(8,128)} %copy.119) | copy-start | bytes 3145732
  226.3 9.1 %copy-start = (f32[64,16,512]{2,1,0:T(8,128)}, f32[64,16,512]{2,1,0:T(8,128)S(1)}, u32[]{:S(2)}) copy-start(f32[64,16,512]{2,1,0:T(8,128)S(1)} %convolution_add_fusion) | copy-start | bytes 6291460
  235.4 1.3 copy-start.2
  239.1 5.6 %copy-start.3 = (f32[64,16,512]{2,1,0:T(8,128)S(1)}, f32[64,16,512]{2,1,0:T(8,128)}, u32[]{:S(2)}) copy-start(f32[64,16,512]{2,1,0:T(8,128)} %copy-done.2) | copy-start | bytes 6291460
  255.0 32.8 %all-to-all-start.5 = ((f32[16,1,16384]{2,1,0:T(1,128)}), f32[16,1,16384]{2,1,0:T(1,128)}, u32[]{:S(2)}, u32[]{:S(2)}) async-start(f32[16,1,16384]{2,1,0:T(1,128)} %reshape.140), calls=%async_computation.5 | async-start | bytes 2097152 | tf_op jit(solution)/shard_map/all_to_all | solution.py:104
  261.0 5.6 %copy-start.1 = (f32[64,16,512]{2,1,0:T(8,128)S(1)}, f32[64,16,512]{2,1,0:T(8,128)}, u32[]{:S(2)}) copy-start(f32[64,16,512]{2,1,0:T(8,128)} %copy-done) | copy-start | bytes 6291460
  287.9 31.2 %all-to-all-start.6 = ((f32[16,1,16384]{2,1,0:T(1,128)}), f32[16,1,16384]{2,1,0:T(1,128)}, u32[]{:S(2)}, u32[]{:S(2)}) async-start(f32[16,1,16384]{2,1,0:T(1,128)} %reshape.142), calls=%async_computation.6 | async-start | bytes 2097152 | tf_op jit(solution)/shard_map/all_to_all | solution.py:105
  328.5 5.5 %copy-start.5 = (f32[64,16,128]{2,1,0:T(8,128)S(1)}, f32[64,16,128]{2,1,0:T(8,128)}, u32[]{:S(2)}) copy-start(f32[64,16,128]{2,1,0:T(8,128)} %fusion.52) | copy-start | bytes 1572868
  335.6 5.5 %copy-start.6 = (f32[64,16,128]{2,1,0:T(8,128)S(1)}, f32[64,16,128]{2,1,0:T(8,128)}, u32[]{:S(2)}) copy-start(f32[64,16,128]{2,1,0:T(8,128)} %fusion.50) | copy-start | bytes 1572868
  337.5 11.6 %all-to-all-start.7 = ((f32[2,1,65536]{2,1,0:T(1,128)}), f32[2,1,65536]{2,1,0:T(1,128)S(1)}, u32[]{:S(2)}, u32[]{:S(2)}) async-start(f32[2,1,65536]{2,1,0:T(1,128)} %reshape.144), calls=%async_computation.7 | async-start | bytes 1048576 | tf_op jit(solution)/shard_map/all_to_all | solution.py:118
  349.1 11.0 %all-to-all-start.8 = ((f32[2,1,65536]{2,1,0:T(1,128)}), f32[2,1,65536]{2,1,0:T(1,128)S(1)}, u32[]{:S(2)}, u32[]{:S(2)}) async-start(f32[2,1,65536]{2,1,0:T(1,128)} %reshape.146), calls=%async_computation.8 | async-start | bytes 1048576 | tf_op jit(solution)/shard_map/all_to_all | solution.py:119
where the time goes:
time: 394 us; the launch traced here: 387 us
  local copies, waits for them, and re-layouts  163 us (41%)
  waiting for transfers between devices  73.2 us (19%)
  matrix products  60 us (15%)
  starting transfers between devices  39.9 us (10%)
  other arithmetic  33.6 us (9%)
  blocking collectives  16 us (4%)
    slice x1, local copies, waits for them, and re-layouts, per_device(): kept_green = jnp.transpose(green[:, :, 0::2], (2, 1, 0))  73.2 us
    dot_general x20, matrix products, product(): return jnp.einsum(form, left, table, precision=lax.Precision.HIGHEST)  60 us
    unnamed x40, local copies, waits for them, and re-layouts  40.5 us
    all_to_all x1, waiting for transfers between devices, per_device(): lax.all_to_all(fy_real, ('gx', 'gz'), split_axis=2, concat_axis=0, tiled=...  18.1 us
    all_to_all x1, blocking collectives, per_device(): return lax.all_to_all(result, 'gz', split_axis=2, concat_axis=0, tiled=True)  16 us
    all_to_all x1, waiting for transfers between devices, per_device(): lax.all_to_all(source, 'gz', split_axis=0, concat_axis=2, tiled=True)  14.5 us
    all_to_all x1, waiting for transfers between devices, per_device(): lax.all_to_all(back_imag, ('gx', 'gz'), split_axis=2, concat_axis=1, tile...  14.2 us
    all_to_all x1, waiting for transfers between devices, per_device(): lax.all_to_all(back_real, ('gx', 'gz'), split_axis=2, concat_axis=1, tile...  13.6 us
  transfers between devices with their start and end apart: 9, of which 8 were waited for; matrix products, arithmetic and copies ran while one was open for 40% of the time, Pallas kernels for 0%

commit v1 on v0

--- a/solution.py
+++ b/solution.py
@@ -1,9 +1,372 @@
+import functools
 import math
 
 import jax
 import jax.numpy as jnp
+import ml_dtypes
+import numpy as np
 from jax import lax
+from jax.experimental import pallas as pl
+from jax.experimental.pallas import tpu as pltpu
 from jax.sharding import PartitionSpec as P
+
+
+LANES = 128
+ALL = ("gx", "gz", "gy")
+MESH = ("gx", "gy", "gz")
+
+
+def np_halves(table):
+    high = table.astype(np.float32).astype(ml_dtypes.bfloat16)
+    low = (table - high.astype(np.float64)).astype(np.float32).astype(ml_dtypes.bfloat16)
+    return np.stack([high, low])
+
+
+def split(value):
+    high = value.astype(jnp.bfloat16)
+    return high, (value - high.astype(jnp.float32)).astype(jnp.bfloat16)
+
+
+def mm(left, right):
+    return jnp.dot(left, right, preferred_element_type=jnp.float32)
+
+
+def table_left(high, low, value):
+    v_high, v_low = split(value)
+    both = mm(high, jnp.concatenate([v_high, v_low], axis=1))
+    width = value.shape[1]
+    return both[:, :width] + (both[:, width:] + mm(low, v_high))
+
+
+def table_right(value, high, low):
+    v_high, v_low = split(value)
+    return mm(v_high, high) + (mm(v_low, high) + mm(v_high, low))
+
+
+def block_swap(pieces, width):
+    count = len(pieces)
+    group = lax.broadcasted_iota(jnp.int32, pieces[0].shape, 1) // width
+    out = []
+    for c in range(count):
+        total = None
+        for g in range(count):
+            moved = pieces[g]
+            shift = (g - c) * width % LANES
+            if shift:
+                moved = pltpu.roll(moved, shift, 1)
+            total = moved if total is None else jnp.where(group == g, moved, total)
+        out.append(total)
+    return out
+
+
+def y_tables(length_y, groups, dests, scale):
+    cells = np.arange(length_y // 2)
+    freq = np.arange(length_y // 2)
+    angle = 2.0 * np.pi * (np.outer(freq, cells) % length_y) / length_y
+    sign = 1.0 - 2.0 * (cells % 2)
+    real, imag = np.cos(angle), -np.sin(angle)
+    imag[0] = sign
+    order = (np.arange(dests)[None, :] * groups + np.arange(groups)[:, None]).reshape(-1)
+    forward = np.concatenate([real[order], imag[order]])
+    weight = np.where(freq == 0, 1.0, 2.0)[:, None] * (scale / length_y)
+    backward = np.concatenate([(real * weight)[order], (imag * weight)[order]]).T
+    return np_halves(forward), np_halves(backward)
+
+
+def x_table(length_x):
+    cells = np.arange(length_x // 4)
+    rows = []
+    for member in range(4):
+        freq = 4 * cells + member
+        angle = 2.0 * np.pi * (np.outer(freq, cells) % length_x) / length_x
+        rows.append(np.concatenate([np.cos(angle), np.sin(angle)], 1))
+    return np_halves(np.stack(rows))
+
+
+def z_table(length_z, parts):
+    place = np.arange(length_z)
+    unit, member = place // 2, place % 2
+    freq = np.where(unit == 0, member * (length_z // 2), np.where(member == 0, unit, length_z - unit))
+    cells = np.arange(length_z // 2)
+    rows = []
+    for freqs in np.split(freq, parts):
+        angle = 2.0 * np.pi * (np.outer(cells, freqs) % length_z) / length_z
+        rows.append(np.concatenate([np.cos(angle), -np.sin(angle)], 1))
+    return np_halves(np.stack(rows))
+
+
+def table_kernel(x_ref, z_ref, x_out, xback_out, z_out, zback_out):
+    for source, out, back in ((x_ref, x_out, xback_out), (z_ref, z_out, zback_out)):
+        size = source.shape[2]
+        for part in range(2):
+            for m in range(source.shape[1]):
+                c = source[part, m, :, :size].astype(jnp.float32)
+                s = source[part, m, :, size:].astype(jnp.float32)
+                full = jnp.concatenate(
+                    [jnp.concatenate([c, s], axis=1), jnp.concatenate([-s, c], axis=1)], axis=0
+                )
+                out[part, m] = full.astype(jnp.bfloat16)
+                back[part, m] = full.T.astype(jnp.bfloat16)
+
+
+def pack_kernel(source_ref, own_ref, sent_ref):
+    group = LANES // source_ref.shape[1]
+    me = lax.axis_index("gy")
+    rows = own_ref.shape[0]
+    for row in range(rows):
+        for half, out_ref in ((me, own_ref), (1 - me, sent_ref)):
+            base = (half * rows + row) * group
+            block = jnp.concatenate([source_ref[base + b] for b in range(group)], axis=0)
+            out_ref[row] = block.T
+
+
+def unpack_kernel(own_ref, other_ref, out_ref):
+    width = out_ref.shape[1]
+    group = LANES // width
+    me = lax.axis_index("gy")
+    rows = own_ref.shape[0]
+    for row in range(rows):
+        for half, in_ref in ((me, own_ref), (1 - me, other_ref)):
+            block = in_ref[row].T
+            for b in range(group):
+                out_ref[(half * rows + row) * group + b] = block[b * width : (b + 1) * width]
+
+
+def green_kernel(units, green_ref, own_ref, sent_ref, nyquist_ref):
+    me = lax.axis_index("gy")
+    positions = 4 * units
+    quarter = own_ref.shape[2]
+    for m in range(4):
+        for u in range(units):
+            for half, out_ref in ((me, own_ref), (1 - me, sent_ref)):
+                at = m * positions + 2 * (half * units + u)
+                out_ref[u, m] = green_ref[pl.ds(at, quarter, stride=4 * positions), :]
+        nyquist_ref[m] = green_ref[pl.ds(m * positions + 1, quarter, stride=4 * positions), :]
+
+
+def y_kernel(dests, width, table_ref, own_ref, other_ref, out_ref):
+    rows = own_ref.shape[0]
+    lower = lax.axis_index("gy") == 0
+    group = LANES // width
+    high, low = table_ref[0], table_ref[1]
+    chunk = 2 * rows * group
+    for a in range(rows):
+        own, other = own_ref[a], other_ref[a]
+        lines = jnp.concatenate(
+            [jnp.where(lower, own, other), jnp.where(lower, other, own)], axis=0
+        )
+        freqs = table_left(high, low, lines)
+        for q in range(2):
+            base = q * group * dests
+            pieces = [freqs[base + c * dests : base + (c + 1) * dests] for c in range(group)]
+            for b, piece in enumerate(block_swap(pieces, width)):
+                start = q * rows * group + a * group + b
+                out_ref[pl.ds(start, dests, stride=chunk), :] = piece
+
+
+def y_back_kernel(dests, width, table_ref, in_ref, own_ref, sent_ref):
+    rows, count_y = own_ref.shape[0], own_ref.shape[1]
+    lower = lax.axis_index("gy") == 0
+    group = LANES // width
+    t_high, t_low = table_ref[0], table_ref[1]
+    chunk = 2 * rows * group
+    for a in range(rows):
+        pieces = []
+        for q in range(2):
+            start = q * rows * group + a * group
+            pieces += block_swap(
+                [in_ref[pl.ds(start + b, dests, stride=chunk), :] for b in range(group)], width
+            )
+        cells = table_left(t_high, t_low, jnp.concatenate(pieces, axis=0))
+        low, high = cells[:count_y], cells[count_y:]
+        own_ref[a] = jnp.where(lower, low, high)
+        sent_ref[a] = jnp.where(lower, high, low)
+
+
+def core_kernel(
+    size_gx, size_gy, size_gz, width,
+    x_ref, xback_ref, z_ref, zback_ref, own_ref, other_ref, nyquist_ref, in_ref, out_ref,
+    lines, spectrum,
+):
+    step = pl.program_id(0)
+    units = LANES // width
+    run = in_ref.shape[2]
+    quarter = x_ref.shape[2] // 2
+    half_x = 2 * quarter
+    me = lax.axis_index("gy")
+    sides = ((0, me, own_ref), (1, 1 - me, other_ref))
+
+    @pl.when(step == 0)
+    def _():
+        for gx in range(size_gx):
+            for gy in range(size_gy):
+                for q in range(2):
+                    pieces = [in_ref[(gx * size_gz + gz) * size_gy + gy, q] for gz in range(size_gz)]
+                    at = q * half_x + (gx * size_gy + gy) * run
+                    for c, piece in enumerate(block_swap(pieces, width)):
+                        lines[c, at : at + run] = piece
+
+    def forward(sign):
+        field = lines[step]
+        r0, r1 = field[:quarter], field[quarter:half_x]
+        i0, i1 = field[half_x : half_x + quarter], field[half_x + quarter :]
+        if sign < 0:
+            i0, i1 = -i0, -i1
+        mixes = [(r0 + r1, i0 + i1), (r0 + i1, i0 - r1), (r0 - r1, i0 - i1), (r0 - i1, i0 + r1)]
+        rows = []
+        for m, (real, imag) in enumerate(mixes):
+            o = table_left(x_ref[0, m], x_ref[1, m], jnp.concatenate([real, imag], axis=0))
+            rows.append(jnp.concatenate([o[:quarter], o[quarter:]], axis=1))
+        rows = jnp.concatenate(rows, axis=0)
+        return [table_right(rows, z_ref[0, h], z_ref[1, h]) for _, h, _ in sides]
+
+    for (side, _, green_ref), freqs in zip(sides, forward(1)):
+        gain = green_ref[0]
+        gain = jnp.where(step == 0, 0.5 * (gain + nyquist_ref[side]), gain)
+        spectrum[side] = jnp.concatenate([gain, gain], axis=1) * freqs
+
+    @pl.when(step == 0)
+    def _():
+        for (side, _, green_ref), freqs in zip(sides, forward(-1)):
+            gain = 0.5 * (green_ref[0] - nyquist_ref[side])
+            spectrum[side] += jnp.concatenate([gain, gain], axis=1) * freqs
+
+    inverse = sum(table_right(spectrum[side], zback_ref[0, h], zback_ref[1, h]) for side, h, _ in sides)
+    near_r = near_i = far_r = far_i = 0.0
+    for m in range(4):
+        rows = inverse[m * quarter : (m + 1) * quarter]
+        both = jnp.concatenate([rows[:, :LANES], rows[:, LANES:]], axis=0)
+        u = table_left(xback_ref[0, m], xback_ref[1, m], both)
+        real, imag = u[:quarter], u[quarter:]
+        near_r, near_i = near_r + real, near_i + imag
+        turn_r, turn_i = [(real, imag), (-imag, real), (-real, -imag), (imag, -real)][m]
+        far_r, far_i = far_r + turn_r, far_i + turn_i
+    lines[step] = jnp.concatenate([near_r, far_r, near_i, far_i], axis=0)
+
+    @pl.when(step == units - 1)
+    def _():
+        for gx in range(size_gx):
+            for gy in range(size_gy):
+                for q in range(2):
+                    at = q * half_x + (gx * size_gy + gy) * run
+                    pieces = [lines[c, at : at + run] for c in range(units)]
+                    for gz, piece in enumerate(block_swap(pieces, width)):
+                        out_ref[(gx * size_gz + gz) * size_gy + gy, q] = piece
+
+
+def call(body, out_shape, *args, **more):
+    return pl.pallas_call(
+        body,
+        out_shape=out_shape,
+        compiler_params=pltpu.CompilerParams(vmem_limit_bytes=48 * 1024 * 1024),
+        **more,
+    )(*args)
+
+
+def f32(*shape):
+    return jax.ShapeDtypeStruct(shape, jnp.float32)
+
+
+def fast_device(source, green):
+    size_gx = lax.axis_size("gx")
+    size_gy = lax.axis_size("gy")
+    size_gz = lax.axis_size("gz")
+    brick_x, brick_y, brick_z = source.shape
+    long_x, places, share = green.shape
+    long_y = 2 * brick_y * size_gy
+    long_z = 2 * brick_z * size_gz
+    dests = size_gx * size_gy * size_gz
+    units = places // (2 * size_gy)
+    group = LANES // brick_z
+    rows = brick_x // size_gy // group
+    run = brick_x // size_gy
+    quarter = long_x // 4
+    y_tab, y_back = y_tables(long_y, units, dests, 1.0 / (long_x * long_z))
+    x_wide = jax.ShapeDtypeStruct((2, 4, 2 * quarter, 2 * quarter), jnp.bfloat16)
+    z_wide = jax.ShapeDtypeStruct((2, 2, long_z, 2 * share), jnp.bfloat16)
+    swap = []
+    for line in range(size_gx):
+        for at in range(size_gz):
+            ends = [(line * size_gy + y) * size_gz + at for y in range(2)]
+            swap += [tuple(ends), tuple(ends[::-1])]
+    exchange = lambda value: lax.ppermute(value, MESH, swap)
+
+    half = f32(rows, brick_y, LANES)
+    own, sent = call(pack_kernel, (half, half), jnp.swapaxes(source, 1, 2))
+    other = exchange(sent)
+
+    slots = f32(units, 4, quarter, share)
+    green_own, green_sent, nyquist = call(
+        functools.partial(green_kernel, units),
+        (slots, slots, f32(4, quarter, share)),
+        green.reshape(long_x * places, share),
+    )
+    own, green_sent, nyquist = lax.optimization_barrier((own, green_sent, nyquist))
+    green_other = exchange(green_sent)
+    green_other = green_other.reshape(units, long_x, share)
+    green_own = green_own.reshape(units, long_x, share)
+    nyquist = nyquist.reshape(long_x, share)
+    distant = lax.ppermute(nyquist, MESH, [(size_gz, 0)])
+    first = jnp.logical_and(
+        lax.axis_index("gx") + lax.axis_index("gz") == 0, lax.axis_index("gy") == 0
+    )
+    nyquist = jnp.stack(
+        [jnp.where(first, nyquist, green_own[0]), jnp.where(first, distant, green_other[0])]
+    )
+
+    sent = call(
+        functools.partial(y_kernel, dests, brick_z),
+        f32(dests * 2 * run, LANES),
+        y_tab,
+        own,
+        other,
+    )
+    sent = sent.reshape(dests, 2, run, LANES)
+    got = lax.all_to_all(sent, ALL, split_axis=0, concat_axis=0, tiled=True)
+    x_tab, x_back, z_tab, z_back = call(
+        table_kernel, (x_wide, x_wide, z_wide, z_wide), x_table(long_x), z_table(long_z, 2)
+    )
+
+    whole = lambda a: pl.BlockSpec(a.shape, lambda c: (0,) * a.ndim)
+    back = call(
+        functools.partial(core_kernel, size_gx, size_gy, size_gz, brick_z),
+        f32(dests, 2, run, LANES),
+        x_tab, x_back, z_tab, z_back, green_own, green_other, nyquist, got,
+        grid=(units,),
+        in_specs=[
+            whole(x_tab), whole(x_back), whole(z_tab), whole(z_back),
+            pl.BlockSpec((1, long_x, share), lambda c: (c, 0, 0)),
+            pl.BlockSpec((1, long_x, share), lambda c: (c, 0, 0)),
+            whole(nyquist), whole(got),
+        ],
+        out_specs=pl.BlockSpec((dests, 2, run, LANES), lambda c: (0, 0, 0, 0)),
+        scratch_shapes=[
+            pltpu.VMEM((units, long_x, LANES), jnp.float32),
+            pltpu.VMEM((2, long_x, 2 * share), jnp.float32),
+        ],
+    )
+    back = lax.all_to_all(back, ALL, split_axis=0, concat_axis=0, tiled=True)
+    own, sent = call(
+        functools.partial(y_back_kernel, dests, brick_z),
+        (half, half),
+        y_back,
+        back.reshape(dests * 2 * run, LANES),
+    )
+    result = call(unpack_kernel, f32(brick_x, brick_z, brick_y), own, exchange(sent))
+    return jnp.swapaxes(result, 1, 2)
+
+
+def fits(sizes, source, green):
+    brick_x, _, brick_z = source.shape
+    units = green.shape[1] // (2 * sizes["gy"])
+    return (
+        brick_z * units == LANES
+        and brick_z * sizes["gz"] == LANES
+        and green.shape[2] == LANES
+        and sizes["gx"] * brick_x == 2 * LANES
+        and brick_x // sizes["gy"] % (LANES // brick_z) == 0
+        and sizes["gy"] == 2
+    )
 
 
 def phase_table(row_index, column_index, length):
@@ -40,6 +403,8 @@
     size_gy = lax.axis_size("gy")
     size_gz = lax.axis_size("gz")
     brick_x, brick_y, brick_z = source.shape
+    if fits({"gx": size_gx, "gy": size_gy, "gz": size_gz}, source, green):
+        return fast_device(source, green)
     grid_x = brick_x * size_gx
     grid_y = brick_y * size_gy
     grid_z = brick_z * size_gz

time: 394 us -> 116 us (0.29); the launches traced: 387 us -> 115 us
  local copies, waits for them, and re-layouts: 163 us -> 5.24 us
  matrix products: 60 us -> 0 us
  waiting for transfers between devices: 73.2 us -> 41.3 us
  other arithmetic: 33.6 us -> 2.47 us
  starting transfers between devices: 39.9 us -> 13.1 us
  Pallas kernels: 0 us -> 23.6 us
  blocking collectives: 16 us -> 29.2 us
    slice x6 -> x2, local copies, waits for them, and re-layouts: 78.6 us -> 1.72 us  [the longest x1 0.97 us: fast_device(): green_other[0]]
    all_to_all x9 -> x1, waiting for transfers between devices: 73.2 us -> 0.01 us  [fast_device(): got = lax.all_to_all(sent, ALL, split_axis=0, concat_axis=0, tiled=True)]
    dot_general x20 -> x0, matrix products: 60 us -> none  [product(): return jnp.einsum(form, left, table, precision=lax.Precision.HIGHEST)]
    ppermute x0 -> x4, waiting for transfers between devices: none -> 41.3 us  [the longest x3 39.5 us: fast_device(): exchange = lambda value: lax.ppermute(value, MESH, swap)]
    unnamed x40 -> x18, local copies, waits for them, and re-layouts: 40.5 us -> 3.51 us
    all_to_all x9 -> x1, starting transfers between devices: 39.9 us -> 6.23 us  [fast_device(): got = lax.all_to_all(sent, ALL, split_axis=0, concat_axis=0, tiled=True)]
    all_to_all x10 -> x0, other arithmetic: 32.6 us -> none  [the longest x1 5.33 us: per_device(): lax.all_to_all(fy_imag, ('gx', 'gz'), split_axis=2, concat_axis=0, tiled=...]
    all_to_all x19 -> x0, local copies, waits for them, and re-layouts: 31.4 us -> none  [the longest x2 7.36 us: per_device(): lax.all_to_all(fy_imag, ('gx', 'gz'), split_axis=2, concat_axis=0, tiled=...]
  transfers between devices with their start and end apart: 9 -> 5, of which waited for: 8 -> 4; matrix products, arithmetic and copies ran while one was open for 40% -> 4% of each run, Pallas kernels for 0% -> 5%
where the time goes in v1:
time: 116 us; the launch traced here: 115 us
  waiting for transfers between devices  41.3 us (36%)
  blocking collectives  29.2 us (25%)
  Pallas kernels  23.6 us (20%)
  starting transfers between devices  13.1 us (11%)
  local copies, waits for them, and re-layouts  5.24 us (5%)
  other arithmetic  2.47 us (2%)
    ppermute x3, waiting for transfers between devices, fast_device(): exchange = lambda value: lax.ppermute(value, MESH, swap)  39.5 us
    all_to_all x1, blocking collectives, fast_device(): back = lax.all_to_all(back, ALL, split_axis=0, concat_axis=0, tiled=True)  29.2 us
    pallas_call x7, Pallas kernels, call(): pl.pallas_call(body, out_shape=out_shape, compiler_params=pltpu.CompilerP...  23.6 us
    all_to_all x1, starting transfers between devices, fast_device(): got = lax.all_to_all(sent, ALL, split_axis=0, concat_axis=0, tiled=True)  6.23 us
    ppermute x3, starting transfers between devices, fast_device(): exchange = lambda value: lax.ppermute(value, MESH, swap)  5.63 us
    unnamed x18, local copies, waits for them, and re-layouts  3.51 us
  transfers between devices with their start and end apart: 5, of which 4 were waited for; matrix products, arithmetic and copies ran while one was open for 4% of the time, Pallas kernels for 5%

profile of v1, /device:TPU:0, one launch (start us, length us, event | category | flops | bytes accessed | tf_op | source)
XLA Modules:
  0.0 115.1 jit_solution(5299388623425720575)
XLA Ops:
  0.0 1.2 %copy-done.2 = f32[64,64,32]{1,2,0:T(8,128)S(1)} copy-done((f32[64,64,32]{1,2,0:T(8,128)S(1)}, f32[64,64,32]{1,2,0:T(8,128)}, u32[]{:S(2)}) %copy-start.2) | copy-done | bytes 524312
  1.2 0.3 shard_map.66
  1.5 3.0 %collective-permute-start.2 = (f32[8,64,128]{2,1,0:T(8,128)S(1)}, f32[8,64,128]{2,1,0:T(8,128)S(1)}, u32[]{:S(2)}, u32[]{:S(2)}) collective-permute-start(f32[8,64,128]{2,1,0:T(8,128)S(1)} %get-tuple-element.30), channel_id=1, source_target_pairs={{0,4},{4,0},{1,5},{5,1},{2,6},{6,2},{3,7},{7,3},{8,12},{12,8},{9,1... | collective-permute-start | bytes 786440 | tf_op jit(solution)/shard_map/ppermute | solution.py:292
  4.6 4.8 %shard_map.65 = (f32[4,4,128,128]{3,2,1,0:T(8,128)S(1)}, f32[4,4,128,128]{3,2,1,0:T(8,128)}, f32[4,128,128]{2,1,0:T(8,128)}) custom-call(f32[8192,128]{1,0:T(8,128)} %bitcast.19), custom_call_target="tpu_custom_call" | custom-call | tf_op jit(solution)/shard_map/pallas_call | solution.py:258
  9.4 1.5 %collective-permute-done.2.other_ref = f32[8,64,128]{2,1,0:T(8,128)S(1)} collective-permute-done((f32[8,64,128]{2,1,0:T(8,128)S(1)}, f32[8,64,128]{2,1,0:T(8,128)S(1)}, u32[]{:S(2)}, u32[]{:S(2)}) %collective-permute-start.2) | collective-permute-done | bytes 262176 | tf_op jit(solution)/shard_map/ppermute | solution.py:292
  10.9 2.6 %shard_map.67 = f32[2048,128]{1,0:T(8,128)} custom-call(bf16[2,256,128]{2,1,0:T(8,128)(2,1)S(1)} %copy-done.8, f32[8,64,128]{2,1,0:T(8,128)S(1)} %get-tuple-element.29.own_ref, f32[8,64,128]{2,1,0:T(8,128)S(1)} %collective-permute-done.2.other_ref), custom_call_target="tpu_custom_call" | custom-call | tf_op jit(solution)/shard_map/pallas_call | solution.py:258
  13.5 6.2 %all-to-all-start = ((f32[32,2,32,128]{3,2,1,0:T(8,128)}), f32[32,2,32,128]{3,2,1,0:T(8,128)}, u32[]{:S(2)}, u32[]{:S(2)}) async-start(f32[32,2,32,128]{3,2,1,0:T(8,128)} %bitcast.9), calls=%async_computation | async-start | bytes 2097152 | tf_op jit(solution)/shard_map/all_to_all | solution.py:325
  19.7 1.8 %collective-permute-start = (f32[4,4,128,128]{3,2,1,0:T(8,128)}, f32[4,4,128,128]{3,2,1,0:T(8,128)}, u32[]{:S(2)}, u32[]{:S(2)}) collective-permute-start(f32[4,4,128,128]{3,2,1,0:T(8,128)} %get-tuple-element.27), channel_id=1, source_target_pairs={{0,4},{4,0},{1,5},{5,1},{2,6},{6,2},{3,7},{7,3},{8,12},{12,8},{9,1... | collective-permute-start | bytes 3145736 | tf_op jit(solution)/shard_map/ppermute | solution.py:292
  21.5 1.3 %collective-permute-start.1 = (f32[512,128]{1,0:T(8,128)}, f32[512,128]{1,0:T(8,128)}, u32[]{:S(2)}, u32[]{:S(2)}) collective-permute-start(f32[512,128]{1,0:T(8,128)} %bitcast.6), channel_id=1, source_target_pairs={{4,0}} | collective-permute-start | bytes 786440 | tf_op jit(solution)/shard_map/ppermute | solution.py:309
  22.8 0.8 slice.8
  23.5 0.4 shard_map.64
  24.0 1.5 %bitcast_select_fusion.1 = f32[1,512,128]{2,1,0:T(8,128)S(1)} fusion(f32[1,4,128,128]{3,2,1,0:T(8,128)} %slice.8, pred[]{:T(512)S(6)} %and.6, f32[1,512,128]{2,1,0:T(8,128)} %bitcast.15), kind=kLoop, calls=%fused_computation.2 | loop fusion | flops 65536 | bytes 786433 | tf_op jit(solution)/shard_map/jit(_where)/select_n | solution.py:314
  25.4 30.8 %collective-permute-done = f32[4,4,128,128]{3,2,1,0:T(8,128)} collective-permute-done((f32[4,4,128,128]{3,2,1,0:T(8,128)}, f32[4,4,128,128]{3,2,1,0:T(8,128)}, u32[]{:S(2)}, u32[]{:S(2)}) %collective-permute-start) | collective-permute-done | bytes 1048608 | tf_op jit(solution)/shard_map/ppermute | solution.py:292
  56.2 1.0 slice.10
  57.2 1.8 %collective-permute-done.1 = f32[512,128]{1,0:T(8,128)} collective-permute-done((f32[512,128]{1,0:T(8,128)}, f32[512,128]{1,0:T(8,128)}, u32[]{:S(2)}, u32[]{:S(2)}) %collective-permute-start.1) | collective-permute-done | bytes 262176 | tf_op jit(solution)/shard_map/ppermute | solution.py:309
  59.0 1.0 bitcast_select_fusion
  60.1 1.2 %copy-done.1 = bf16[2,4,256,256]{3,2,1,0:T(8,128)(2,1)S(1)} copy-done((bf16[2,4,256,256]{3,2,1,0:T(8,128)(2,1)S(1)}, bf16[2,4,256,256]{3,2,1,0:T(8,128)(2,1)}, u32[]{:S(2)}) %copy-start.1) | copy-done | bytes 1048600
  61.3 1.0 copy-done.5
  62.4 13.0 %shard_map.68 = f32[32,2,32,128]{3,2,1,0:T(8,128)S(1)} custom-call(bf16[2,4,256,256]{3,2,1,0:T(8,128)(2,1)S(1)} %get-tuple-element.19.x_ref, bf16[2,4,256,256]{3,2,1,0:T(8,128)(2,1)S(1)} %copy-done.1, bf16[2,2,256,256]{3,2,1,0:T(8,128)(2,1)S(1)} %get-tuple-element.21.z_ref, bf16[2,2,256,256]{3,2,1,0:T(8,128)(2,1)S(1)} %copy-done.5, ...), custom_call_target="tpu_custom_call" | custom-call | tf_op jit(solution)/shard_map/pallas_call | solution.py:258
  75.4 29.2 %all_to_all.10 = f32[32,2,32,128]{3,2,1,0:T(8,128)S(1)} all-to-all(f32[32,2,32,128]{3,2,1,0:T(8,128)S(1)} %shard_map.68), channel_id=1, replica_groups=mesh['gx'=4,'gy'=2,'gz'=4] {'gx','gz','gy'}, dimensions={0} | all-to-all | bytes 2097152 | tf_op jit(solution)/shard_map/all_to_all | solution.py:348
  104.6 1.2 %shard_map.69 = (f32[8,64,128]{2,1,0:T(8,128)S(1)}, f32[8,64,128]{2,1,0:T(8,128)S(1)}) custom-call(bf16[2,128,256]{2,1,0:T(8,128)(2,1)S(1)} %copy-done.7, f32[2048,128]{1,0:T(8,128)S(1)} %bitcast.16), custom_call_target="tpu_custom_call" | custom-call | tf_op jit(solution)/shard_map/pallas_call | solution.py:258
  105.8 0.8 collective-permute-start.3
  106.6 7.2 %collective-permute-done.3.other_ref = f32[8,64,128]{2,1,0:T(8,128)S(1)} collective-permute-done((f32[8,64,128]{2,1,0:T(8,128)S(1)}, f32[8,64,128]{2,1,0:T(8,128)S(1)}, u32[]{:S(2)}, u32[]{:S(2)}) %collective-permute-start.3) | collective-permute-done | bytes 262176 | tf_op jit(solution)/shard_map/ppermute | solution.py:292
  113.8 1.3 %shard_map.70 = f32[64,32,64]{2,1,0:T(8,128)} custom-call(f32[8,64,128]{2,1,0:T(8,128)S(1)} %get-tuple-element.31.own_ref, f32[8,64,128]{2,1,0:T(8,128)S(1)} %collective-permute-done.3.other_ref), custom_call_target="tpu_custom_call" | custom-call | tf_op jit(solution)/shard_map/pallas_call | solution.py:258
  (17 shorter events, 0.1 us)
Async XLA Ops:
  0.0 1.2 %copy-start.2 = (f32[64,64,32]{1,2,0:T(8,128)S(1)}, f32[64,64,32]{1,2,0:T(8,128)}, u32[]{:S(2)}) copy-start(f32[64,64,32]{1,2,0:T(8,128)} %param.6) | copy-start | bytes 1572868
  1.2 9.7 %copy-start.8 = (bf16[2,256,128]{2,1,0:T(8,128)(2,1)S(1)}, bf16[2,256,128]{2,1,0:T(8,128)(2,1)}, u32[]{:S(2)}) copy-start(bf16[2,256,128]{2,1,0:T(8,128)(2,1)} %constant.22.clone.table_ref) | copy-start | bytes 393220
  1.5 9.3 %collective-permute-start.2 = (f32[8,64,128]{2,1,0:T(8,128)S(1)}, f32[8,64,128]{2,1,0:T(8,128)S(1)}, u32[]{:S(2)}, u32[]{:S(2)}) collective-permute-start(f32[8,64,128]{2,1,0:T(8,128)S(1)} %get-tuple-element.30), channel_id=1, source_target_pairs={{0,4},{4,0},{1,5},{5,1},{2,6},{6,2},{3,7},{7,3},{8,12},{12,8},{9,1... | collective-permute-start | bytes 786440 | tf_op jit(solution)/shard_map/ppermute | solution.py:292
  4.6 19.0 %copy-start.3 = (bf16[2,4,128,256]{3,2,1,0:T(8,128)(2,1)S(1)}, bf16[2,4,128,256]{3,2,1,0:T(8,128)(2,1)}, u32[]{:S(2)}) copy-start(bf16[2,4,128,256]{3,2,1,0:T(8,128)(2,1)} %constant.23.clone.x_ref) | copy-start | bytes 1572868
  4.6 19.0 %copy-start.6 = (bf16[2,2,128,256]{3,2,1,0:T(8,128)(2,1)S(1)}, bf16[2,2,128,256]{3,2,1,0:T(8,128)(2,1)}, u32[]{:S(2)}) copy-start(bf16[2,2,128,256]{3,2,1,0:T(8,128)(2,1)} %constant.24.clone.z_ref) | copy-start | bytes 786436
  13.5 46.6 %all-to-all-start = ((f32[32,2,32,128]{3,2,1,0:T(8,128)}), f32[32,2,32,128]{3,2,1,0:T(8,128)}, u32[]{:S(2)}, u32[]{:S(2)}) async-start(f32[32,2,32,128]{3,2,1,0:T(8,128)} %bitcast.9), calls=%async_computation | async-start | bytes 2097152 | tf_op jit(solution)/shard_map/all_to_all | solution.py:325
  19.7 36.5 %collective-permute-start = (f32[4,4,128,128]{3,2,1,0:T(8,128)}, f32[4,4,128,128]{3,2,1,0:T(8,128)}, u32[]{:S(2)}, u32[]{:S(2)}) collective-permute-start(f32[4,4,128,128]{3,2,1,0:T(8,128)} %get-tuple-element.27), channel_id=1, source_target_pairs={{0,4},{4,0},{1,5},{5,1},{2,6},{6,2},{3,7},{7,3},{8,12},{12,8},{9,1... | collective-permute-start | bytes 3145736 | tf_op jit(solution)/shard_map/ppermute | solution.py:292
  21.5 37.6 %collective-permute-start.1 = (f32[512,128]{1,0:T(8,128)}, f32[512,128]{1,0:T(8,128)}, u32[]{:S(2)}, u32[]{:S(2)}) collective-permute-start(f32[512,128]{1,0:T(8,128)} %bitcast.6), channel_id=1, source_target_pairs={{4,0}} | collective-permute-start | bytes 786440 | tf_op jit(solution)/shard_map/ppermute | solution.py:309
  23.9 36.1 %copy-start = (bf16[2,4,256,256]{3,2,1,0:T(8,128)(2,1)}, bf16[2,4,256,256]{3,2,1,0:T(8,128)(2,1)S(1)}, u32[]{:S(2)}) copy-start(bf16[2,4,256,256]{3,2,1,0:T(8,128)(2,1)S(1)} %get-tuple-element.20.xback_ref) | copy-start | bytes 3145732
  24.0 36.1 %copy-start.4 = (bf16[2,2,256,256]{3,2,1,0:T(8,128)(2,1)}, bf16[2,2,256,256]{3,2,1,0:T(8,128)(2,1)S(1)}, u32[]{:S(2)}) copy-start(bf16[2,2,256,256]{3,2,1,0:T(8,128)(2,1)S(1)} %get-tuple-element.22.zback_ref) | copy-start | bytes 1572868
  60.1 1.2 %copy-start.1 = (bf16[2,4,256,256]{3,2,1,0:T(8,128)(2,1)S(1)}, bf16[2,4,256,256]{3,2,1,0:T(8,128)(2,1)}, u32[]{:S(2)}) copy-start(bf16[2,4,256,256]{3,2,1,0:T(8,128)(2,1)} %copy-done) | copy-start | bytes 3145732
  61.3 1.0 copy-start.5
  62.4 42.2 %copy-start.7 = (bf16[2,128,256]{2,1,0:T(8,128)(2,1)S(1)}, bf16[2,128,256]{2,1,0:T(8,128)(2,1)}, u32[]{:S(2)}) copy-start(bf16[2,128,256]{2,1,0:T(8,128)(2,1)} %constant.25.clone.table_ref) | copy-start | bytes 393220
  105.8 8.0 %collective-permute-start.3 = (f32[8,64,128]{2,1,0:T(8,128)S(1)}, f32[8,64,128]{2,1,0:T(8,128)S(1)}, u32[]{:S(2)}, u32[]{:S(2)}) collective-permute-start(f32[8,64,128]{2,1,0:T(8,128)S(1)} %get-tuple-element.32), channel_id=1, source_target_pairs={{0,4},{4,0},{1,5},{5,1},{2,6},{6,2},{3,7},{7,3},{8,12},{12,8},{9,1... | collective-permute-start | bytes 786440 | tf_op jit(solution)/shard_map/ppermute | solution.py:292

commit v2 on v1

--- a/solution.py
+++ b/solution.py
@@ -185,7 +185,7 @@
 
 def core_kernel(
     size_gx, size_gy, size_gz, width,
-    x_ref, xback_ref, z_ref, zback_ref, own_ref, other_ref, nyquist_ref, in_ref, out_ref,
+    x_ref, xback_ref, z_ref, zback_ref, own_ref, other_ref, nyquist_ref, distant_ref, in_ref, out_ref,
     lines, spectrum,
 ):
     step = pl.program_id(0)
@@ -195,6 +195,10 @@
     half_x = 2 * quarter
     me = lax.axis_index("gy")
     sides = ((0, me, own_ref), (1, 1 - me, other_ref))
+    alternates = (nyquist_ref, distant_ref)
+    packed = jnp.logical_and(
+        step == 0, lax.axis_index("gx") + lax.axis_index("gz") + me == 0
+    )
 
     @pl.when(step == 0)
     def _():
@@ -222,13 +226,13 @@
 
     for (side, _, green_ref), freqs in zip(sides, forward(1)):
         gain = green_ref[0]
-        gain = jnp.where(step == 0, 0.5 * (gain + nyquist_ref[side]), gain)
+        gain = jnp.where(packed, 0.5 * (gain + alternates[side][...]), gain)
         spectrum[side] = jnp.concatenate([gain, gain], axis=1) * freqs
 
-    @pl.when(step == 0)
+    @pl.when(packed)
     def _():
         for (side, _, green_ref), freqs in zip(sides, forward(-1)):
-            gain = 0.5 * (green_ref[0] - nyquist_ref[side])
+            gain = 0.5 * (green_ref[0] - alternates[side][...])
             spectrum[side] += jnp.concatenate([gain, gain], axis=1) * freqs
 
     inverse = sum(table_right(spectrum[side], zback_ref[0, h], zback_ref[1, h]) for side, h, _ in sides)
@@ -307,12 +311,6 @@
     green_own = green_own.reshape(units, long_x, share)
     nyquist = nyquist.reshape(long_x, share)
     distant = lax.ppermute(nyquist, MESH, [(size_gz, 0)])
-    first = jnp.logical_and(
-        lax.axis_index("gx") + lax.axis_index("gz") == 0, lax.axis_index("gy") == 0
-    )
-    nyquist = jnp.stack(
-        [jnp.where(first, nyquist, green_own[0]), jnp.where(first, distant, green_other[0])]
-    )
 
     sent = call(
         functools.partial(y_kernel, dests, brick_z),
@@ -331,13 +329,13 @@
     back = call(
         functools.partial(core_kernel, size_gx, size_gy, size_gz, brick_z),
         f32(dests, 2, run, LANES),
-        x_tab, x_back, z_tab, z_back, green_own, green_other, nyquist, got,
+        x_tab, x_back, z_tab, z_back, green_own, green_other, nyquist, distant, got,
         grid=(units,),
         in_specs=[
             whole(x_tab), whole(x_back), whole(z_tab), whole(z_back),
             pl.BlockSpec((1, long_x, share), lambda c: (c, 0, 0)),
             pl.BlockSpec((1, long_x, share), lambda c: (c, 0, 0)),
-            whole(nyquist), whole(got),
+            whole(nyquist), whole(distant), whole(got),
         ],
         out_specs=pl.BlockSpec((dests, 2, run, LANES), lambda c: (0, 0, 0, 0)),
         scratch_shapes=[

time: 116 us -> 116 us (level)
  local copies, waits for them, and re-layouts: 5.24 us -> 8.55 us
  other arithmetic: 2.47 us -> 0 us
    ppermute x1, waiting for transfers between devices: 1.84 us -> 32.2 us  [fast_device(): distant = lax.ppermute(nyquist, MESH, [(size_gz, 0)])]
    ppermute x3, waiting for transfers between devices: 39.5 us -> 9.32 us  [fast_device(): exchange = lambda value: lax.ppermute(value, MESH, swap)]
    unnamed x18 -> x22, local copies, waits for them, and re-layouts: 3.51 us -> 8.55 us
    select_n x2 -> x0, other arithmetic: 2.43 us -> none  [the longest x1 1.46 us: fast_device(): jnp.where(first, nyquist, green_own[0])]
    slice x2 -> x0, local copies, waits for them, and re-layouts: 1.72 us -> none  [the longest x1 0.97 us: fast_device(): green_other[0]]
  transfers between devices with their start and end apart: 5 -> 5, of which waited for: 4 -> 3; matrix products, arithmetic and copies ran while one was open for 4% -> 0% of each run, Pallas kernels for 5% -> 4%
where the time goes in v2:
time: 116 us
  waiting for transfers between devices  41.5 us (36%)
  blocking collectives  29.2 us (25%)
  Pallas kernels  23 us (20%)
  starting transfers between devices  13.1 us (11%)
  local copies, waits for them, and re-layouts  8.55 us (7%)
    ppermute x1, waiting for transfers between devices, fast_device(): distant = lax.ppermute(nyquist, MESH, [(size_gz, 0)])  32.2 us
    all_to_all x1, blocking collectives, fast_device(): back = lax.all_to_all(back, ALL, split_axis=0, concat_axis=0, tiled=True)  29.2 us
    pallas_call x7, Pallas kernels, call(): pl.pallas_call(body, out_shape=out_shape, compiler_params=pltpu.CompilerP...  23 us
    ppermute x3, waiting for transfers between devices, fast_device(): exchange = lambda value: lax.ppermute(value, MESH, swap)  9.32 us
    unnamed x22, local copies, waits for them, and re-layouts  8.55 us
    all_to_all x1, starting transfers between devices, fast_device(): got = lax.all_to_all(sent, ALL, split_axis=0, concat_axis=0, tiled=True)  6.23 us
    ppermute x3, starting transfers between devices, fast_device(): exchange = lambda value: lax.ppermute(value, MESH, swap)  5.63 us
  transfers between devices with their start and end apart: 5, of which 3 were waited for; matrix products, arithmetic and copies ran while one was open for 0% of the time, Pallas kernels for 4%

profile of v2, /device:TPU:0, one launch (start us, length us, event | category | flops | bytes accessed | tf_op | source)
XLA Modules:
  0.0 115.5 jit_solution(15953571108465502898)
XLA Ops:
  0.0 1.2 %copy-done = f32[64,64,32]{1,2,0:T(8,128)S(1)} copy-done((f32[64,64,32]{1,2,0:T(8,128)S(1)}, f32[64,64,32]{1,2,0:T(8,128)}, u32[]{:S(2)}) %copy-start) | copy-done | bytes 524312
  1.5 3.0 %collective-permute-start.2 = (f32[8,64,128]{2,1,0:T(8,128)S(1)}, f32[8,64,128]{2,1,0:T(8,128)S(1)}, u32[]{:S(2)}, u32[]{:S(2)}) collective-permute-start(f32[8,64,128]{2,1,0:T(8,128)S(1)} %get-tuple-element.30), channel_id=1, source_target_pairs={{0,4},{4,0},{1,5},{5,1},{2,6},{6,2},{3,7},{7,3},{8,12},{12,8},{9,1... | collective-permute-start | bytes 786440 | tf_op jit(solution)/shard_map/ppermute | solution.py:296
  4.6 4.2 %shard_map.65 = (f32[4,4,128,128]{3,2,1,0:T(8,128)S(1)}, f32[4,4,128,128]{3,2,1,0:T(8,128)}, f32[4,128,128]{2,1,0:T(8,128)S(1)}) custom-call(f32[8192,128]{1,0:T(8,128)} %bitcast.13), custom_call_target="tpu_custom_call" | custom-call | tf_op jit(solution)/shard_map/pallas_call | solution.py:262
  8.8 2.1 %collective-permute-done.2.other_ref = f32[8,64,128]{2,1,0:T(8,128)S(1)} collective-permute-done((f32[8,64,128]{2,1,0:T(8,128)S(1)}, f32[8,64,128]{2,1,0:T(8,128)S(1)}, u32[]{:S(2)}, u32[]{:S(2)}) %collective-permute-start.2) | collective-permute-done | bytes 262176 | tf_op jit(solution)/shard_map/ppermute | solution.py:296
  10.9 2.6 %shard_map.67 = f32[2048,128]{1,0:T(8,128)} custom-call(bf16[2,256,128]{2,1,0:T(8,128)(2,1)S(1)} %copy-done.10, f32[8,64,128]{2,1,0:T(8,128)S(1)} %get-tuple-element.29.own_ref, f32[8,64,128]{2,1,0:T(8,128)S(1)} %collective-permute-done.2.other_ref), custom_call_target="tpu_custom_call" | custom-call | tf_op jit(solution)/shard_map/pallas_call | solution.py:262
  13.5 6.2 %all-to-all-start = ((f32[32,2,32,128]{3,2,1,0:T(8,128)}), f32[32,2,32,128]{3,2,1,0:T(8,128)}, u32[]{:S(2)}, u32[]{:S(2)}) async-start(f32[32,2,32,128]{3,2,1,0:T(8,128)} %bitcast.5), calls=%async_computation | async-start | bytes 2097152 | tf_op jit(solution)/shard_map/all_to_all | solution.py:323
  19.7 1.8 %collective-permute-start = (f32[4,4,128,128]{3,2,1,0:T(8,128)}, f32[4,4,128,128]{3,2,1,0:T(8,128)}, u32[]{:S(2)}, u32[]{:S(2)}) collective-permute-start(f32[4,4,128,128]{3,2,1,0:T(8,128)} %get-tuple-element.27), channel_id=1, source_target_pairs={{0,4},{4,0},{1,5},{5,1},{2,6},{6,2},{3,7},{7,3},{8,12},{12,8},{9,1... | collective-permute-start | bytes 3145736 | tf_op jit(solution)/shard_map/ppermute | solution.py:296
  21.5 1.3 %collective-permute-start.1 = (f32[512,128]{1,0:T(8,128)S(1)}, f32[512,128]{1,0:T(8,128)S(1)}, u32[]{:S(2)}, u32[]{:S(2)}) collective-permute-start(f32[512,128]{1,0:T(8,128)S(1)} %bitcast.11), channel_id=1, source_target_pairs={{4,0}} | collective-permute-start | bytes 786440 | tf_op jit(solution)/shard_map/ppermute | solution.py:313
  22.8 1.0 copy-done.1
  23.8 0.9 copy-done.6
  24.8 0.4 shard_map.64
  25.2 0.8 copy-done.2
  26.0 0.8 copy-done.4
  26.8 32.2 %collective-permute-done.1.distant_ref = f32[512,128]{1,0:T(8,128)S(1)} collective-permute-done((f32[512,128]{1,0:T(8,128)S(1)}, f32[512,128]{1,0:T(8,128)S(1)}, u32[]{:S(2)}, u32[]{:S(2)}) %collective-permute-start.1) | collective-permute-done | bytes 262176 | tf_op jit(solution)/shard_map/ppermute | solution.py:313
  58.9 0.7 copy-done.7
  59.7 1.0 copy-done.3
  60.7 1.0 copy-done.5
  61.8 0.9 copy-done.8
  62.7 13.0 %shard_map.68 = f32[32,2,32,128]{3,2,1,0:T(8,128)S(1)} custom-call(bf16[2,4,256,256]{3,2,1,0:T(8,128)(2,1)S(1)} %get-tuple-element.19.x_ref, bf16[2,4,256,256]{3,2,1,0:T(8,128)(2,1)S(1)} %get-tuple-element.20.xback_ref, bf16[2,2,256,256]{3,2,1,0:T(8,128)(2,1)S(1)} %copy-done.3, bf16[2,2,256,256]{3,2,1,0:T(8,128)(2,1)S(1)} %copy-done.5, ...), custom_call_target="tpu_custom_call" | custom-call | tf_op jit(solution)/shard_map/pallas_call | solution.py:262
  75.8 29.2 %all_to_all.10 = f32[32,2,32,128]{3,2,1,0:T(8,128)S(1)} all-to-all(f32[32,2,32,128]{3,2,1,0:T(8,128)S(1)} %shard_map.68), channel_id=1, replica_groups=mesh['gx'=4,'gy'=2,'gz'=4] {'gx','gz','gy'}, dimensions={0} | all-to-all | bytes 2097152 | tf_op jit(solution)/shard_map/all_to_all | solution.py:346
  105.0 1.2 %shard_map.69 = (f32[8,64,128]{2,1,0:T(8,128)S(1)}, f32[8,64,128]{2,1,0:T(8,128)S(1)}) custom-call(bf16[2,128,256]{2,1,0:T(8,128)(2,1)S(1)} %copy-done.9, f32[2048,128]{1,0:T(8,128)S(1)} %bitcast.8), custom_call_target="tpu_custom_call" | custom-call | tf_op jit(solution)/shard_map/pallas_call | solution.py:262
  106.2 0.8 collective-permute-start.3
  107.0 7.2 %collective-permute-done.3.other_ref = f32[8,64,128]{2,1,0:T(8,128)S(1)} collective-permute-done((f32[8,64,128]{2,1,0:T(8,128)S(1)}, f32[8,64,128]{2,1,0:T(8,128)S(1)}, u32[]{:S(2)}, u32[]{:S(2)}) %collective-permute-start.3) | collective-permute-done | bytes 262176 | tf_op jit(solution)/shard_map/ppermute | solution.py:296
  114.2 1.3 %shard_map.70 = f32[64,32,64]{2,1,0:T(8,128)} custom-call(f32[8,64,128]{2,1,0:T(8,128)S(1)} %get-tuple-element.31.own_ref, f32[8,64,128]{2,1,0:T(8,128)S(1)} %collective-permute-done.3.other_ref), custom_call_target="tpu_custom_call" | custom-call | tf_op jit(solution)/shard_map/pallas_call | solution.py:262
  (16 shorter events, 0.3 us)
Async XLA Ops:
  0.0 1.2 %copy-start = (f32[64,64,32]{1,2,0:T(8,128)S(1)}, f32[64,64,32]{1,2,0:T(8,128)}, u32[]{:S(2)}) copy-start(f32[64,64,32]{1,2,0:T(8,128)} %param.6) | copy-start | bytes 1572868
  1.2 9.7 %copy-start.10 = (bf16[2,256,128]{2,1,0:T(8,128)(2,1)S(1)}, bf16[2,256,128]{2,1,0:T(8,128)(2,1)}, u32[]{:S(2)}) copy-start(bf16[2,256,128]{2,1,0:T(8,128)(2,1)} %constant.8.clone.table_ref) | copy-start | bytes 393220
  1.5 9.3 %collective-permute-start.2 = (f32[8,64,128]{2,1,0:T(8,128)S(1)}, f32[8,64,128]{2,1,0:T(8,128)S(1)}, u32[]{:S(2)}, u32[]{:S(2)}) collective-permute-start(f32[8,64,128]{2,1,0:T(8,128)S(1)} %get-tuple-element.30), channel_id=1, source_target_pairs={{0,4},{4,0},{1,5},{5,1},{2,6},{6,2},{3,7},{7,3},{8,12},{12,8},{9,1... | collective-permute-start | bytes 786440 | tf_op jit(solution)/shard_map/ppermute | solution.py:296
  13.5 46.2 %all-to-all-start = ((f32[32,2,32,128]{3,2,1,0:T(8,128)}), f32[32,2,32,128]{3,2,1,0:T(8,128)}, u32[]{:S(2)}, u32[]{:S(2)}) async-start(f32[32,2,32,128]{3,2,1,0:T(8,128)} %bitcast.5), calls=%async_computation | async-start | bytes 2097152 | tf_op jit(solution)/shard_map/all_to_all | solution.py:323
  19.7 40.0 %collective-permute-start = (f32[4,4,128,128]{3,2,1,0:T(8,128)}, f32[4,4,128,128]{3,2,1,0:T(8,128)}, u32[]{:S(2)}, u32[]{:S(2)}) collective-permute-start(f32[4,4,128,128]{3,2,1,0:T(8,128)} %get-tuple-element.27), channel_id=1, source_target_pairs={{0,4},{4,0},{1,5},{5,1},{2,6},{6,2},{3,7},{7,3},{8,12},{12,8},{9,1... | collective-permute-start | bytes 3145736 | tf_op jit(solution)/shard_map/ppermute | solution.py:296
  21.5 37.5 %collective-permute-start.1 = (f32[512,128]{1,0:T(8,128)S(1)}, f32[512,128]{1,0:T(8,128)S(1)}, u32[]{:S(2)}, u32[]{:S(2)}) collective-permute-start(f32[512,128]{1,0:T(8,128)S(1)} %bitcast.11), channel_id=1, source_target_pairs={{4,0}} | collective-permute-start | bytes 786440 | tf_op jit(solution)/shard_map/ppermute | solution.py:313
  22.8 1.0 copy-start.1
  23.8 0.9 copy-start.6
  25.2 0.8 copy-start.2
  26.0 0.8 copy-start.4
  58.9 0.7 copy-start.7
  59.7 1.0 copy-start.3
  60.7 1.0 copy-start.5
  61.8 0.9 copy-start.8
  62.7 42.3 %copy-start.9 = (bf16[2,128,256]{2,1,0:T(8,128)(2,1)S(1)}, bf16[2,128,256]{2,1,0:T(8,128)(2,1)}, u32[]{:S(2)}) copy-start(bf16[2,128,256]{2,1,0:T(8,128)(2,1)} %constant.11.clone.table_ref) | copy-start | bytes 393220
  106.2 8.0 %collective-permute-start.3 = (f32[8,64,128]{2,1,0:T(8,128)S(1)}, f32[8,64,128]{2,1,0:T(8,128)S(1)}, u32[]{:S(2)}, u32[]{:S(2)}) collective-permute-start(f32[8,64,128]{2,1,0:T(8,128)S(1)} %get-tuple-element.32), channel_id=1, source_target_pairs={{0,4},{4,0},{1,5},{5,1},{2,6},{6,2},{3,7},{7,3},{8,12},{12,8},{9,1... | collective-permute-start | bytes 786440 | tf_op jit(solution)/shard_map/ppermute | solution.py:296
